TPU v7x, 32 devices: a whole 2x2x4 slice. The times are simulated.
32 devices in a mesh: dev: 8 (over y, x, core), ka: 4 (over z).
Axes of the slice: x: 2, y: 2, z: 4, core: 2. Of those that a mesh axis runs over, the one named last changes fastest.
Arguments:
- tile_data: float32 [2048, 128, 128], P(('dev', 'ka')), may hold values from -0.25 to 0.25
- tile_row: int32 [32, 64], P(('dev', 'ka')), may hold values from 0 to 31
- tile_col: int32 [32, 64], P(('dev', 'ka')), may hold values from 0 to 63
- tile_count: int32 [32], P(('dev', 'ka')), may hold values from 10 to 64, as said below
- touched: int32 [32, 64], P(('dev', 'ka')), may hold values from 0 to 127, as said below
- owner_map: int32 [128], replicated, may hold values from 0 to 127, as said below
- observed: float32 [1024, 128, 64], P(('dev', 'ka')), may hold values from -6 to 6
- start_x: float32 [2048, 128, 64], P(('dev', 'ka')), may hold values from -6 to 6
- start_u: float32 [2048, 128, 64], P(('dev', 'ka')), may hold values from -4 to 4
Outputs:
- final_x: float32 [2048, 128, 64], P(('dev', 'ka'))
- final_u: float32 [2048, 128, 64], P(('dev', 'ka'))
- z_keeper_agreed: float32 [128, 128, 64], P(('dev', 'ka'))
- primal_gap: float32 [64], replicated
Inputs may be any that keep to these rules, and one draw needn't show every extreme that they name: Shard s uses its first tile_count[s] slots; each count is at least 10 and at most 64, and some shard has exactly 64. `touched`: A shard's 64 entries are distinct column blocks. The owner of block j is shard owner_map[j] // 4; a shard touches at most 2 blocks of one owner, and every shard touches exactly 2 blocks of some owner. `owner_map`: A permutation of 0 to 127.
All inputs are finite; a program needn't handle non-finite values.
Results may differ from a plain program's by a relative error of at most 0.0003.
Values sent between devices are 32-bit elements.
A program may use at most 128 MiB of HBM per device.

v0:
```python
import functools
import math

import jax
import jax.numpy as jnp
from jax import lax
from jax.experimental import pallas as pl
from jax.experimental.pallas import tpu as pltpu
from jax.sharding import PartitionSpec as P

ITERS = 2
CG_STEPS = 4
PENALTY = 1.0
COUPLING = 1.0
AXES = ("dev", "ka")
MESH = pl.DeviceIdType.MESH
MIB = 1 << 20


def vmem():
    return pl.BlockSpec(memory_space=pltpu.VMEM)


def smem():
    return pl.BlockSpec(memory_space=pltpu.SMEM)


def split(value):
    high = value.astype(jnp.bfloat16)
    low = (value - high.astype(jnp.float32)).astype(jnp.bfloat16)
    return jnp.concatenate([high, low], axis=0)


def tile_pass(tiles_ref, from_ids, to_ids, in_count, source_ref, target_ref):
    group = math.gcd(16, tiles_ref.shape[0])
    half = source_ref.shape[1] // 2

    def add_group(number, carry):
        for inner in range(group):
            t = number * group + inner
            lhs = source_ref[from_ids[0, t]]
            out = jnp.dot(
                jnp.concatenate([lhs, lhs], axis=1),
                tiles_ref[t],
                preferred_element_type=jnp.float32,
            )
            landing = to_ids[0, t]
            target_ref[landing] = target_ref[landing] + (out[:half] + out[half:])
        return carry

    lax.fori_loop(0, (in_count + group - 1) // group, add_group, 0)


def fill_zero(ref):
    def one(i, carry):
        ref[i] = jnp.zeros(ref.shape[1:], ref.dtype)
        return carry

    lax.fori_loop(0, ref.shape[0], one, 0, unroll=4)


def lanes(total):
    return jnp.sum(total, axis=1, keepdims=True)


def prepare_kernel(
    rows, cols, count, mailbox, tile_ref, obs_ref, x_ref, u_ref,
    fwd_ref, bwd_ref, base_ref, box_ref, xb_ref, w_ref, wb_ref,
):
    in_count = count[0]
    slots = tile_ref.shape[0]
    local_cols, targets, blk = x_ref.shape

    if box_ref.shape[0] != local_cols:
        fill_zero(box_ref)

    def convert(t, carry):
        tile = jnp.where(t < in_count, tile_ref[t], 0.0)
        bwd_ref[t] = split(tile)
        fwd_ref[t] = split(tile.T)
        return carry

    lax.fori_loop(0, slots, convert, 0, unroll=4)

    def begin(c, carry):
        x = x_ref[c]
        box_ref[mailbox[0, c]] = x + u_ref[c]
        xb_ref[c] = split(x)
        base_ref[c] = -x * COUPLING
        return carry

    lax.fori_loop(0, local_cols, begin, 0, unroll=4)
    fill_zero(w_ref)
    tile_pass(fwd_ref, cols, rows, in_count, xb_ref, w_ref)

    def against(r, carry):
        wb_ref[r] = split(obs_ref[r] - w_ref[r])
        return carry

    lax.fori_loop(0, w_ref.shape[0], against, 0, unroll=4)
    tile_pass(bwd_ref, rows, cols, in_count, wb_ref, base_ref)


def solve_kernel(
    last, rows, cols, count, mailbox, fwd_ref, bwd_ref, base_ref, x_ref, u_ref, zbox_ref,
    newx_ref, newu_ref, *rest,
):
    if last:
        gap_ref, r_ref, p_ref, q_ref, pb_ref, w_ref, wb_ref = rest
    else:
        box_ref, r_ref, p_ref, q_ref, pb_ref, w_ref, wb_ref = rest
    in_count = count[0]
    local_cols, targets, blk = x_ref.shape
    row_blocks = w_ref.shape[0]
    zero = jnp.zeros((targets, blk), jnp.float32)

    def begin(c, carry):
        rr, gap = carry
        z = zbox_ref[mailbox[0, c]]
        d = x_ref[c] - z
        u = u_ref[c] + d
        newu_ref[c] = u
        newx_ref[c] = x_ref[c]
        r = base_ref[c] + COUPLING * (z - u)
        r_ref[c] = r
        p_ref[c] = r
        q_ref[c] = COUPLING * r
        pb_ref[c] = split(r)
        return rr + r * r, gap + d * d

    rr, gap = lax.fori_loop(0, local_cols, begin, (zero, zero), unroll=2)
    if last:
        gap_ref[...] = gap
    rr = lanes(rr)
    pp = rr
    for step in range(CG_STEPS):
        final = last and step == CG_STEPS - 1
        fill_zero(w_ref)
        tile_pass(fwd_ref, cols, rows, in_count, pb_ref, w_ref)

        def image(i, ww):
            w = w_ref[i]
            if not final:
                wb_ref[i] = split(w)
            return ww + w * w

        ww = lanes(lax.fori_loop(0, row_blocks, image, zero, unroll=4))
        size = rr / (ww + COUPLING * pp)
        if final:

            def finish(c, carry):
                newx_ref[c] = newx_ref[c] + size * p_ref[c]
                return carry

            lax.fori_loop(0, local_cols, finish, 0, unroll=4)
            break
        tile_pass(bwd_ref, rows, cols, in_count, wb_ref, q_ref)

        def reduce(c, total):
            r = r_ref[c] - size * q_ref[c]
            r_ref[c] = r
            return total + r * r

        if step == CG_STEPS - 1:

            def close(c, carry):
                x = newx_ref[c] + size * p_ref[c]
                newx_ref[c] = x
                r = r_ref[c] - size * q_ref[c]
                slot = mailbox[0, c]
                u = newu_ref[c]
                box_ref[slot] = x + u
                base_ref_out[c] = r - COUPLING * (zbox_ref[slot] - u)
                return carry

            base_ref_out = r_ref
            if box_ref.shape[0] != local_cols:
                fill_zero(box_ref)
            lax.fori_loop(0, local_cols, close, 0, unroll=2)
            break
        norm = lanes(lax.fori_loop(0, local_cols, reduce, zero, unroll=4))
        turn = norm / rr

        def direct(c, total):
            old = p_ref[c]
            newx_ref[c] = newx_ref[c] + size * old
            p = r_ref[c] + turn * old
            p_ref[c] = p
            q_ref[c] = COUPLING * p
            pb_ref[c] = split(p)
            return total + p * p

        pp = lanes(lax.fori_loop(0, local_cols, direct, zero, unroll=2))
        rr = norm


def agree_kernel(
    first, n, capacity, col_dev, box_ref, tag_ref, zbox_ref, zown_ref, *rest
):
    if first:
        got_ref, inbox, ans, send, recv, send_back, recv_back, tag_send, tag_recv = rest
    else:
        inbox, ans, send, recv, send_back, recv_back = rest
        got_ref = tag_ref
    ka = lax.axis_size(AXES[1])
    me = lax.axis_index(AXES[0]) * ka + lax.axis_index(AXES[1])

    def place(device):
        return (device // ka, lax.rem(device, ka))

    def after(i):
        return lax.rem(me + i, n)

    def before(i):
        return lax.rem(me + n - i, n)

    def tags_to(i):
        return pltpu.make_async_remote_copy(
            tag_ref.at[after(i)], got_ref.at[me], tag_send.at[i], tag_recv.at[i],
            device_id=place(after(i)), device_id_type=MESH,
        )

    def tags_from(i):
        return pltpu.make_async_remote_copy(
            tag_ref.at[before(i)], got_ref.at[before(i)], tag_send.at[i], tag_recv.at[i],
            device_id=place(before(i)), device_id_type=MESH,
        )

    def part(device):
        return pl.ds(device * capacity, capacity)

    def copy(i, source, target, send_sem, recv_sem):
        return pltpu.make_async_remote_copy(
            source.at[part(after(i))], target.at[part(me)], send_sem.at[i], recv_sem.at[i],
            device_id=place(after(i)), device_id_type=MESH,
        )

    def arrival(i, source, target, send_sem, recv_sem):
        return pltpu.make_async_remote_copy(
            source.at[part(before(i))], target.at[part(before(i))], send_sem.at[i],
            recv_sem.at[i], device_id=place(before(i)), device_id_type=MESH,
        )

    def start(i, carry):
        if first:
            tags_to(i).start()
        copy(i, box_ref, inbox, send, recv).start()
        return carry

    lax.fori_loop(1, n, start, 0)
    if first:
        got_ref[me] = tag_ref[me]

    def take(source_ref, device, sums):
        counts = []
        for j in range(capacity):
            value = source_ref[device * capacity + j]
            tag = got_ref[device, pl.ds(j, 1)]
            for k in range(col_dev):
                zown_ref[k] = zown_ref[k] + jnp.where(tag == k, value, 0.0)
                counts.append((k, jnp.where(tag == k, 1.0, 0.0)))
        sums = list(sums)
        for k, hit in counts:
            sums[k] = sums[k] + hit
        return tuple(sums)

    for k in range(col_dev):
        zown_ref[k] = jnp.zeros(zown_ref.shape[1:], jnp.float32)
    none = jnp.zeros((1, zown_ref.shape[2]), jnp.float32)
    shares = take(box_ref, me, (none,) * col_dev)

    def collect(i, shares):
        if first:
            tags_from(i).wait_recv()
        arrival(i, box_ref, inbox, send, recv).wait_recv()
        return take(inbox, before(i), shares)

    shares = lax.fori_loop(1, n, collect, shares)
    for k in range(col_dev):
        share = jnp.maximum(shares[k], 1.0)
        amount = zown_ref[k] / share
        cutoff = PENALTY / (COUPLING * share)
        zown_ref[k] = amount - jnp.clip(amount, -cutoff, cutoff)

    def answer(device, target_ref):
        for j in range(capacity):
            tag = got_ref[device, pl.ds(j, 1)]
            value = jnp.zeros(zown_ref.shape[1:], jnp.float32)
            for k in range(col_dev):
                value = value + jnp.where(tag == k, zown_ref[k], 0.0)
            target_ref[device * capacity + j] = value

    def reply(i, carry):
        answer(after(i), ans)
        copy(i, ans, zbox_ref, send_back, recv_back).start()
        return carry

    lax.fori_loop(1, n, reply, 0)
    answer(me, zbox_ref)

    def settle(i, carry):
        arrival(i, ans, zbox_ref, send_back, recv_back).wait_recv()
        copy(i, ans, zbox_ref, send_back, recv_back).wait_send()
        copy(i, box_ref, inbox, send, recv).wait_send()
        if first:
            tags_to(i).wait_send()
        return carry

    lax.fori_loop(1, n, settle, 0)


def on_device(
    tile_data, tile_row, tile_col, tile_count, touched, owner_map, observed, start_x, start_u
):
    shards = lax.axis_size(AXES)
    local_cols = touched.shape[1]
    col_blocks = owner_map.shape[0]
    col_dev = col_blocks // shards
    capacity = max(1, (local_cols + shards - 1) // shards)
    row_blocks = observed.shape[0]
    slots, blk, _ = tile_data.shape
    targets = start_x.shape[2]
    boxes = shards * capacity
    f32, b16 = jnp.float32, jnp.bfloat16
    shape = jax.ShapeDtypeStruct

    wanted = touched[0]
    matches = (wanted[:, None] == jnp.arange(col_blocks, dtype=jnp.int32)[None, :]).astype(
        jnp.int32
    )
    position = jnp.sum(matches * owner_map[None, :], axis=1)
    owner = position // col_dev
    local_slot = position - owner * col_dev
    slot_order = jnp.arange(local_cols, dtype=jnp.int32)
    earlier = (owner[:, None] == owner[None, :]) & (slot_order[:, None] > slot_order[None, :])
    mailbox = owner * capacity + jnp.sum(earlier.astype(jnp.int32), axis=1)
    hit = mailbox[:, None] == jnp.arange(boxes, dtype=jnp.int32)[None, :]
    tags = jnp.sum(jnp.where(hit, local_slot[:, None] + 1, 0), axis=0) - 1
    tag_rows = -(-capacity // 8) * 8
    tags = jnp.pad(
        tags.astype(f32).reshape(shards, capacity),
        ((0, 0), (0, tag_rows - capacity)),
        constant_values=-1.0,
    )
    tags = jnp.broadcast_to(tags[:, :, None], (shards, tag_rows, blk))
    mailbox = mailbox[None, :]

    x = jnp.swapaxes(start_x, 1, 2)
    u = jnp.swapaxes(start_u, 1, 2)
    obs = jnp.swapaxes(observed, 1, 2)
    vec = (local_cols, targets, blk)
    big = 40 * MIB

    fwd, bwd, base, box = pl.pallas_call(
        prepare_kernel,
        out_shape=(
            shape((slots, 2 * blk, blk), b16),
            shape((slots, 2 * blk, blk), b16),
            shape(vec, f32),
            shape((boxes, targets, blk), f32),
        ),
        in_specs=[smem()] * 4 + [vmem()] * 4,
        out_specs=(vmem(),) * 4,
        scratch_shapes=[
            pltpu.VMEM((local_cols, 2 * targets, blk), b16),
            pltpu.VMEM((row_blocks, targets, blk), f32),
            pltpu.VMEM((row_blocks, 2 * targets, blk), b16),
        ],
        compiler_params=pltpu.CompilerParams(vmem_limit_bytes=big),
        name="prepare",
    )(tile_row, tile_col, tile_count, mailbox, tile_data, obs, x, u)

    def agree(first, box, tags):
        outs = [shape((boxes, targets, blk), f32), shape((col_dev, targets, blk), f32)]
        sems = [pltpu.SemaphoreType.DMA((shards,))] * 4
        if first:
            outs.append(shape(tags.shape, f32))
            sems = sems + [pltpu.SemaphoreType.DMA((shards,))] * 2
        return pl.pallas_call(
            functools.partial(agree_kernel, first, shards, capacity, col_dev),
            out_shape=tuple(outs),
            in_specs=[vmem()] * 2,
            out_specs=(vmem(),) * len(outs),
            scratch_shapes=[
                pltpu.VMEM((boxes, targets, blk), f32),
                pltpu.VMEM((boxes, targets, blk), f32),
            ] + sems,
            compiler_params=pltpu.CompilerParams(
                vmem_limit_bytes=big, has_side_effects=True
            ),
            name="agree",
        )(box, tags)

    for outer_step in range(ITERS):
        first, last = outer_step == 0, outer_step == ITERS - 1
        if first:
            zbox, zown, tags = agree(True, box, tags)
        else:
            zbox, zown = agree(False, box, tags)
        common = [
            pltpu.VMEM(vec, f32),
            pltpu.VMEM(vec, f32),
            pltpu.VMEM((local_cols, 2 * targets, blk), b16),
            pltpu.VMEM((row_blocks, targets, blk), f32),
            pltpu.VMEM((row_blocks, 2 * targets, blk), b16),
        ]
        if last:
            outs = (shape(vec, f32), shape(vec, f32), shape((targets, blk), f32))
            common = [pltpu.VMEM(vec, f32)] + common
        else:
            outs = (
                shape(vec, f32), shape(vec, f32), shape((boxes, targets, blk), f32),
                shape(vec, f32),
            )
        result = pl.pallas_call(
            functools.partial(solve_kernel, last),
            out_shape=outs,
            in_specs=[smem()] * 4 + [vmem()] * 6,
            out_specs=(vmem(),) * len(outs),
            scratch_shapes=common,
            compiler_params=pltpu.CompilerParams(vmem_limit_bytes=big),
            name="solve",
        )(tile_row, tile_col, tile_count, mailbox, fwd, bwd, base, x, u, zbox)
        if last:
            x, u, gap = result
        else:
            x, u, box, base = result
    gap_total = lax.psum(jnp.sum(gap, axis=1), AXES)
    primal_gap = jnp.sqrt(gap_total / (shards * local_cols * blk))
    return (jnp.swapaxes(x, 1, 2), jnp.swapaxes(u, 1, 2), jnp.swapaxes(zown, 1, 2), primal_gap)


def solution(mesh):
    both = P(AXES)
    placed = (
        P(AXES, None, None), P(AXES, None), P(AXES, None), both, P(AXES, None), P(),
        P(AXES, None, None), P(AXES, None, None), P(AXES, None, None),
    )
    return jax.shard_map(
        on_device,
        mesh=mesh,
        in_specs=placed,
        out_specs=(P(AXES, None, None), P(AXES, None, None), P(AXES, None, None), P()),
        check_vma=False,
    )
```

profile of v0, /device:TPU:0, one launch (start us, length us, event | category | flops | bytes accessed | tf_op | source)
XLA Modules:
  0.0 315.8 jit_solution(17068454362847624318)
XLA Ops:
  1.3 0.8 select_reduce_fusion.1
  2.2 0.2 convert_reduce_fusion
  2.4 0.1 select_reduce_fusion
  2.5 0.1 convert_element_type.13
  2.6 0.1 broadcast_in_dim.12.tag_ref
  2.7 0.0 copy-start.2
  2.7 1.6 copy-done.2
  4.3 0.0 copy-start.4
  4.3 1.6 copy-done.4
  5.9 0.0 copy-start.8
  5.9 1.2 copy-done.8
  7.1 0.0 copy-start.9
  7.1 0.7 copy-done.9
  7.8 0.0 copy-start.10
  7.8 0.7 copy-done.10
  8.4 8.8 %prepare.1 = (bf16[64,256,128]{2,1,0:T(8,128)(2,1)S(1)}, bf16[64,256,128]{2,1,0:T(8,128)(2,1)}, f32[64,64,128]{2,1,0:T(8,128)S(1)}, f32[64,64,128]{2,1,0:T(8,128)S(1)}) custom-call(s32[1,64]{1,0:T(1,128)S(1)} %copy-done.9, s32[1,64]{1,0:T(1,128)S(1)} %copy-done.10, s32[1]{0:T(128)S(6)} %copy.14.count, s32[1,64]{1,0:T(1,128)S(1)} %bitcast_add_fusion.mailbox, ...), custom_call_target="tpu_custom_call" | custom-call | tf_op jit(solution)/shard_map/prepare/pallas_call | solution.py:354
  17.3 0.0 copy-start
  17.3 2.0 copy-done
  19.2 0.0 copy-start.5
  19.2 0.0 copy-start.3
  19.2 104.0 %agree.2 = (f32[64,64,128]{2,1,0:T(8,128)S(1)}, f32[4,64,128]{2,1,0:T(8,128)}, f32[32,8,128]{2,1,0:T(8,128)S(1)}) custom-call(f32[64,64,128]{2,1,0:T(8,128)S(1)} %get-tuple-element.22.box_ref, f32[32,8,128]{2,1,0:T(8,128)S(1)} %broadcast_in_dim.12.tag_ref), custom_call_target="tpu_custom_call" | custom-call | tf_op jit(solution)/shard_map/agree/pallas_call | solution.py:379
  123.3 0.0 copy-start.7
  123.3 1.3 copy-done.7
  124.6 0.0 copy-done.5
  124.6 0.0 copy-done.3
  124.6 0.0 copy-start.6
  124.6 1.6 copy-done.6
  126.2 0.0 copy-start.1
  126.2 19.4 %solve.2 = (f32[64,64,128]{2,1,0:T(8,128)S(1)}, f32[64,64,128]{2,1,0:T(8,128)S(1)}, f32[64,64,128]{2,1,0:T(8,128)S(1)}, f32[64,64,128]{2,1,0:T(8,128)S(1)}) custom-call(s32[1,64]{1,0:T(1,128)S(1)} %copy-done.9, s32[1,64]{1,0:T(1,128)S(1)} %copy-done.10, s32[1]{0:T(128)S(6)} %copy.14.count, s32[1,64]{1,0:T(1,128)S(1)} %bitcast_add_fusion.mailbox, ...), custom_call_target="tpu_custom_call" | custom-call | tf_op jit(solution)/shard_map/solve/pallas_call | solution.py:415
  145.6 104.7 %agree.3 = (f32[64,64,128]{2,1,0:T(8,128)S(1)}, f32[4,64,128]{2,1,0:T(8,128)S(1)}) custom-call(f32[64,64,128]{2,1,0:T(8,128)S(1)} %get-tuple-element.27.box_ref, f32[32,8,128]{2,1,0:T(8,128)S(1)} %get-tuple-element.28.tag_ref), custom_call_target="tpu_custom_call" | custom-call | tf_op jit(solution)/shard_map/agree/pallas_call | solution.py:379
  250.3 0.0 copy-done.1
  250.3 17.2 %solve.3 = (f32[64,64,128]{2,1,0:T(8,128)}, f32[64,64,128]{2,1,0:T(8,128)}, f32[64,128]{1,0:T(8,128)S(1)}) custom-call(s32[1,64]{1,0:T(1,128)S(1)} %copy-done.9, s32[1,64]{1,0:T(1,128)S(1)} %copy-done.10, s32[1]{0:T(128)S(6)} %copy.14.count, s32[1,64]{1,0:T(1,128)S(1)} %bitcast_add_fusion.mailbox, bf16[64,256,128]{2,1,0:T(8,128)(2,1)S(1)} %copy-done.1, ...), custom_call_target="tpu_custom_call" | custom-call | tf_op jit(solution)/shard_map/solve/pallas_call | solution.py:415
  267.4 0.1 reduce_sum.45
  267.6 47.0 %psum.7 = f32[64]{0:T(128)S(1)} all-reduce(f32[64]{0:T(128)S(1)} %reduce_sum.45), channel_id=1, replica_groups=mesh['dev'=8,'ka'=4] {'dev','ka'}, use_global_device_ids=true, to_apply=%region_4.5 | all-reduce | flops 64 | bytes 512 | tf_op jit(solution)/shard_map/psum | solution.py:428
  314.6 0.5 multiply_sqrt_fusion
  315.1 0.7 copy.15
  (5 shorter events, 0.0 us)
Async XLA Ops:
  2.7 1.6 copy-start.2
  4.3 1.6 copy-start.4
  5.9 1.2 copy-start.8
  7.1 0.7 copy-start.9
  7.8 0.7 copy-start.10
  17.3 2.0 copy-start
  19.2 105.4 %copy-start.5 = (f32[64,64,128]{2,1,0:T(8,128)}, f32[64,64,128]{2,1,0:T(8,128)S(1)}, u32[]{:S(2)}) copy-start(f32[64,64,128]{2,1,0:T(8,128)S(1)} %get-tuple-element.21.base_ref) | copy-start | bytes 6291460
  19.2 105.4 %copy-start.3 = (f32[64,128,64]{1,2,0:T(8,128)S(1)}, f32[64,128,64]{1,2,0:T(8,128)}, u32[]{:S(2)}) copy-start(f32[64,128,64]{1,2,0:T(8,128)} %param.16) | copy-start | bytes 6291460
  123.3 1.3 copy-start.7
  124.6 1.6 copy-start.6
  126.2 124.1 %copy-start.1 = (bf16[64,256,128]{2,1,0:T(8,128)(2,1)S(1)}, bf16[64,256,128]{2,1,0:T(8,128)(2,1)}, u32[]{:S(2)}) copy-start(bf16[64,256,128]{2,1,0:T(8,128)(2,1)} %copy-done) | copy-start | bytes 12582916
where the time goes:
time: 321 us; the launch traced here: 316 us
  Pallas kernels  254 us (79%)
  blocking collectives  47 us (15%)
  local copies, waits for them, and re-layouts  11.5 us (4%)
    pallas_call x2, Pallas kernels, agree(): pl.pallas_call(functools.partial(agree_kernel, first, shards, capacity, c...  209 us
    psum x1, blocking collectives, on_device(): gap_total = lax.psum(jnp.sum(gap, axis=1), AXES)  47 us
    pallas_call x2, Pallas kernels, on_device(): pl.pallas_call(functools.partial(solve_kernel, last), out_shape=outs, in_...  36.5 us
    unnamed x23, local copies, waits for them, and re-layouts  11.3 us
    pallas_call x1, Pallas kernels, on_device(): pl.pallas_call(prepare_kernel, out_shape=(shape((slots, 2 * blk, blk), b1...  8.85 us

commit v1 on v0

--- a/solution.py
+++ b/solution.py
@@ -106,7 +106,7 @@
     newx_ref, newu_ref, *rest,
 ):
     if last:
-        gap_ref, r_ref, p_ref, q_ref, pb_ref, w_ref, wb_ref = rest
+        r_ref, p_ref, q_ref, pb_ref, w_ref, wb_ref = rest
     else:
         box_ref, r_ref, p_ref, q_ref, pb_ref, w_ref, wb_ref = rest
     in_count = count[0]
@@ -114,8 +114,7 @@
     row_blocks = w_ref.shape[0]
     zero = jnp.zeros((targets, blk), jnp.float32)
 
-    def begin(c, carry):
-        rr, gap = carry
+    def begin(c, rr):
         z = zbox_ref[mailbox[0, c]]
         d = x_ref[c] - z
         u = u_ref[c] + d
@@ -126,12 +125,9 @@
         p_ref[c] = r
         q_ref[c] = COUPLING * r
         pb_ref[c] = split(r)
-        return rr + r * r, gap + d * d
-
-    rr, gap = lax.fori_loop(0, local_cols, begin, (zero, zero), unroll=2)
-    if last:
-        gap_ref[...] = gap
-    rr = lanes(rr)
+        return rr + r * r
+
+    rr = lanes(lax.fori_loop(0, local_cols, begin, zero, unroll=2))
     pp = rr
     for step in range(CG_STEPS):
         final = last and step == CG_STEPS - 1
@@ -194,119 +190,270 @@
         rr = norm
 
 
-def agree_kernel(
-    first, n, capacity, col_dev, box_ref, tag_ref, zbox_ref, zown_ref, *rest
-):
+def agree_kernel(first, last, capacity, col_dev, mean_of, *refs):
+    refs = list(refs)
+    box_ref, tag_ref = refs.pop(0), refs.pop(0)
+    if not first:
+        share_ref = refs.pop(0)
+    if last:
+        mailbox, x_ref = refs.pop(0), refs.pop(0)
+    zbox_ref, zown_ref = refs.pop(0), refs.pop(0)
     if first:
-        got_ref, inbox, ans, send, recv, send_back, recv_back, tag_send, tag_recv = rest
+        got_ref, share_ref = refs.pop(0), refs.pop(0)
     else:
-        inbox, ans, send, recv, send_back, recv_back = rest
         got_ref = tag_ref
-    ka = lax.axis_size(AXES[1])
-    me = lax.axis_index(AXES[0]) * ka + lax.axis_index(AXES[1])
-
-    def place(device):
-        return (device // ka, lax.rem(device, ka))
+    if last:
+        gap_ref = refs.pop(0)
+    inbox, ans, part_ref, far_ref, zall_ref = refs[:5]
+    send, recv, back_send, back_recv, far_send, far_recv, all_send, all_recv = refs[5:13]
+    refs = refs[13:]
+    if first:
+        count_ref, far_count, tag_send, tag_recv, count_send, count_recv = refs
+    if last:
+        gaps, gap_send, gap_recv = refs
+
+    nd, nk = lax.axis_size(AXES[0]), lax.axis_size(AXES[1])
+    n = nd * nk
+    md, mk = lax.axis_index(AXES[0]), lax.axis_index(AXES[1])
 
     def after(i):
-        return lax.rem(me + i, n)
+        return lax.rem(md + i, nd)
 
     def before(i):
-        return lax.rem(me + n - i, n)
+        return lax.rem(md + nd - i, nd)
+
+    def remote(source, target, send_sem, recv_sem, device):
+        return pltpu.make_async_remote_copy(
+            source, target, send_sem, recv_sem, device_id=device, device_id_type=MESH
+        )
+
+    def cell(d, k):
+        return pl.ds((d * nk + k) * capacity, capacity)
+
+    def tags_of(d):
+        return pl.ds(d * nk, nk)
 
     def tags_to(i):
-        return pltpu.make_async_remote_copy(
-            tag_ref.at[after(i)], got_ref.at[me], tag_send.at[i], tag_recv.at[i],
-            device_id=place(after(i)), device_id_type=MESH,
+        return remote(
+            tag_ref.at[tags_of(after(i))], got_ref.at[tags_of(md)],
+            tag_send.at[i], tag_recv.at[i], (after(i), mk),
         )
 
     def tags_from(i):
-        return pltpu.make_async_remote_copy(
-            tag_ref.at[before(i)], got_ref.at[before(i)], tag_send.at[i], tag_recv.at[i],
-            device_id=place(before(i)), device_id_type=MESH,
-        )
-
-    def part(device):
-        return pl.ds(device * capacity, capacity)
-
-    def copy(i, source, target, send_sem, recv_sem):
-        return pltpu.make_async_remote_copy(
-            source.at[part(after(i))], target.at[part(me)], send_sem.at[i], recv_sem.at[i],
-            device_id=place(after(i)), device_id_type=MESH,
-        )
-
-    def arrival(i, source, target, send_sem, recv_sem):
-        return pltpu.make_async_remote_copy(
-            source.at[part(before(i))], target.at[part(before(i))], send_sem.at[i],
-            recv_sem.at[i], device_id=place(before(i)), device_id_type=MESH,
-        )
-
-    def start(i, carry):
+        return remote(
+            tag_ref.at[tags_of(before(i))], got_ref.at[tags_of(before(i))],
+            tag_send.at[i], tag_recv.at[i], (before(i), mk),
+        )
+
+    def plane_to(i, k, source, target, sems):
+        return remote(
+            source.at[cell(after(i), k)], target.at[cell(md, k)],
+            sems[0].at[i, k], sems[1].at[i, k], (after(i), mk),
+        )
+
+    def plane_from(i, k, source, target, sems):
+        return remote(
+            source.at[cell(before(i), k)], target.at[cell(before(i), k)],
+            sems[0].at[i, k], sems[1].at[i, k], (before(i), mk),
+        )
+
+    there, back = (send, recv), (back_send, back_recv)
+
+    def blocks(k):
+        return pl.ds(k * col_dev, col_dev)
+
+    def to_owner(o):
+        k = lax.rem(mk + o, nk)
+        return remote(
+            part_ref.at[blocks(k)], far_ref.at[blocks(o)], far_send.at[o], far_recv.at[o],
+            (md, k),
+        )
+
+    def count_to_owner(o):
+        k = lax.rem(mk + o, nk)
+        return remote(
+            count_ref.at[k], far_count.at[o], count_send.at[o], count_recv.at[o], (md, k)
+        )
+
+    def from_owner(o):
+        k = lax.rem(mk + o, nk)
+        return remote(
+            zown_ref, zall_ref.at[blocks(nk - o)], all_send.at[o], all_recv.at[o], (md, k)
+        )
+
+    order = list(range(1, nk)) + [0]
+    if first:
+
+        def start_tags(i, carry):
+            tags_to(i).start()
+            return carry
+
+        lax.fori_loop(1, nd, start_tags, 0)
+    for o in order:
+        k = lax.rem(mk + o, nk)
+
+        def start(i, carry):
+            plane_to(i, k, box_ref, inbox, there).start()
+            return carry
+
+        lax.fori_loop(1, nd, start, 0)
+    if first:
+        got_ref[tags_of(md)] = tag_ref[tags_of(md)]
+        count_ref[...] = jnp.zeros_like(count_ref)
+    part_ref[...] = jnp.zeros_like(part_ref)
+
+    def take(source_ref, d, k):
+        for j in range(capacity):
+            value = source_ref[(d * nk + k) * capacity + j]
+            tag = got_ref[d * nk + k, pl.ds(j, 1)]
+            for b in range(col_dev):
+                at = k * col_dev + b
+                part_ref[at] = part_ref[at] + jnp.where(tag == b, value, 0.0)
+                if first:
+                    spot = pl.ds(b, 1)
+                    count_ref[k, spot] = count_ref[k, spot] + jnp.where(tag == b, 1.0, 0.0)
+
+    for position, o in enumerate(order):
+        k = lax.rem(mk + o, nk)
+        take(box_ref, md, k)
+
+        def collect(i, carry):
+            if first and position == 0:
+                tags_from(i).wait_recv()
+            plane_from(i, k, box_ref, inbox, there).wait_recv()
+            take(inbox, before(i), k)
+            return carry
+
+        lax.fori_loop(1, nd, collect, 0)
+        if o:
+            to_owner(o).start()
+            if first:
+                count_to_owner(o).start()
+
+    for b in range(col_dev):
+        zown_ref[b] = part_ref[mk * col_dev + b]
+    if first:
+        share_ref[...] = count_ref[mk]
+    for o in range(1, nk):
+        to_owner(o).wait_recv()
+        for b in range(col_dev):
+            zown_ref[b] = zown_ref[b] + far_ref[o * col_dev + b]
         if first:
-            tags_to(i).start()
-        copy(i, box_ref, inbox, send, recv).start()
-        return carry
-
-    lax.fori_loop(1, n, start, 0)
-    if first:
-        got_ref[me] = tag_ref[me]
-
-    def take(source_ref, device, sums):
-        counts = []
+            count_to_owner(o).wait_recv()
+            share_ref[...] = share_ref[...] + far_count[o]
+    for b in range(col_dev):
+        share = jnp.maximum(share_ref[pl.ds(b, 1)], 1.0)
+        amount = zown_ref[b] / share
+        cutoff = PENALTY / (COUPLING * share)
+        z = amount - jnp.clip(amount, -cutoff, cutoff)
+        zown_ref[b] = z
+        zall_ref[b] = z
+    for o in range(1, nk):
+        from_owner(o).start()
+
+    def answer(d, k, slot, target_ref):
         for j in range(capacity):
-            value = source_ref[device * capacity + j]
-            tag = got_ref[device, pl.ds(j, 1)]
-            for k in range(col_dev):
-                zown_ref[k] = zown_ref[k] + jnp.where(tag == k, value, 0.0)
-                counts.append((k, jnp.where(tag == k, 1.0, 0.0)))
-        sums = list(sums)
-        for k, hit in counts:
-            sums[k] = sums[k] + hit
-        return tuple(sums)
-
-    for k in range(col_dev):
-        zown_ref[k] = jnp.zeros(zown_ref.shape[1:], jnp.float32)
-    none = jnp.zeros((1, zown_ref.shape[2]), jnp.float32)
-    shares = take(box_ref, me, (none,) * col_dev)
-
-    def collect(i, shares):
-        if first:
-            tags_from(i).wait_recv()
-        arrival(i, box_ref, inbox, send, recv).wait_recv()
-        return take(inbox, before(i), shares)
-
-    shares = lax.fori_loop(1, n, collect, shares)
-    for k in range(col_dev):
-        share = jnp.maximum(shares[k], 1.0)
-        amount = zown_ref[k] / share
-        cutoff = PENALTY / (COUPLING * share)
-        zown_ref[k] = amount - jnp.clip(amount, -cutoff, cutoff)
-
-    def answer(device, target_ref):
-        for j in range(capacity):
-            tag = got_ref[device, pl.ds(j, 1)]
-            value = jnp.zeros(zown_ref.shape[1:], jnp.float32)
-            for k in range(col_dev):
-                value = value + jnp.where(tag == k, zown_ref[k], 0.0)
-            target_ref[device * capacity + j] = value
-
-    def reply(i, carry):
-        answer(after(i), ans)
-        copy(i, ans, zbox_ref, send_back, recv_back).start()
-        return carry
-
-    lax.fori_loop(1, n, reply, 0)
-    answer(me, zbox_ref)
-
-    def settle(i, carry):
-        arrival(i, ans, zbox_ref, send_back, recv_back).wait_recv()
-        copy(i, ans, zbox_ref, send_back, recv_back).wait_send()
-        copy(i, box_ref, inbox, send, recv).wait_send()
-        if first:
-            tags_to(i).wait_send()
-        return carry
-
-    lax.fori_loop(1, n, settle, 0)
+            tag = got_ref[d * nk + k, pl.ds(j, 1)]
+            value = jnp.where(tag == 0, zall_ref[slot * col_dev], 0.0)
+            for b in range(1, col_dev):
+                value = value + jnp.where(tag == b, zall_ref[slot * col_dev + b], 0.0)
+            target_ref[(d * nk + k) * capacity + j] = value
+
+    for o in range(nk):
+        k = lax.rem(mk + o, nk)
+        if o:
+            from_owner(nk - o).wait_recv()
+
+        def reply(i, carry):
+            answer(after(i), k, o, ans)
+            plane_to(i, k, ans, zbox_ref, back).start()
+            return carry
+
+        lax.fori_loop(1, nd, reply, 0)
+        answer(md, k, o, zbox_ref)
+
+    for o in range(nk):
+        k = lax.rem(mk + o, nk)
+
+        def settle(i, carry):
+            plane_from(i, k, ans, zbox_ref, back).wait_recv()
+            return carry
+
+        lax.fori_loop(1, nd, settle, 0)
+
+    if last:
+        me = md * nk + mk
+
+        def gap_to(i):
+            device = lax.rem(me + i, n)
+            return remote(
+                gaps.at[me], gaps.at[me], gap_send.at[i], gap_recv.at[i],
+                (device // nk, lax.rem(device, nk)),
+            )
+
+        def gap_from(i):
+            device = lax.rem(me + n - i, n)
+            return remote(
+                gaps.at[device], gaps.at[device], gap_send.at[i], gap_recv.at[i],
+                (device // nk, lax.rem(device, nk)),
+            )
+
+        targets, blk = x_ref.shape[1:]
+
+        def square(c, total):
+            d = x_ref[c] - zbox_ref[mailbox[0, c]]
+            return total + d * d
+
+        zero = jnp.zeros((targets, blk), jnp.float32)
+        total = lax.fori_loop(0, x_ref.shape[0], square, zero)
+        width = gaps.shape[2]
+        if width > targets:
+            total = jnp.concatenate(
+                [total, jnp.zeros((width - targets, blk), jnp.float32)], axis=0
+            )
+        gaps[me] = lax.dot_general(
+            jnp.ones((8, blk), jnp.float32), total, (((1,), (1,)), ((), ())),
+            precision=lax.Precision.HIGHEST, preferred_element_type=jnp.float32,
+        )
+
+        def tell(i, carry):
+            gap_to(i).start()
+            return carry
+
+        lax.fori_loop(1, n, tell, 0)
+
+        def heard(i, carry):
+            gap_from(i).wait_recv()
+            return carry
+
+        lax.fori_loop(1, n, heard, 0)
+        whole = lax.fori_loop(
+            0, n, lambda i, t: t + gaps[i], jnp.zeros((8, width), jnp.float32)
+        )
+        gap_ref[...] = jnp.sqrt(whole / mean_of)
+
+        def told(i, carry):
+            gap_to(i).wait_send()
+            return carry
+
+        lax.fori_loop(1, n, told, 0)
+
+    for o in range(nk):
+        k = lax.rem(mk + o, nk)
+
+        def sent(i, carry):
+            plane_to(i, k, box_ref, inbox, there).wait_send()
+            plane_to(i, k, ans, zbox_ref, back).wait_send()
+            if first and o == 0:
+                tags_to(i).wait_send()
+            return carry
+
+        lax.fori_loop(1, nd, sent, 0)
+        if o:
+            to_owner(o).wait_send()
+            from_owner(o).wait_send()
+            if first:
+                count_to_owner(o).wait_send()
 
 
 def on_device(
@@ -370,33 +517,54 @@
         name="prepare",
     )(tile_row, tile_col, tile_count, mailbox, tile_data, obs, x, u)
 
-    def agree(first, box, tags):
+    nd, nk = lax.axis_size(AXES[0]), lax.axis_size(AXES[1])
+    count_rows = -(-col_dev // 8) * 8
+    width = -(-targets // blk) * blk
+    dma = pltpu.SemaphoreType.DMA
+
+    def agree(first, last, *operands):
         outs = [shape((boxes, targets, blk), f32), shape((col_dev, targets, blk), f32)]
-        sems = [pltpu.SemaphoreType.DMA((shards,))] * 4
+        specs = [vmem()] * len(operands)
+        dense = pltpu.VMEM((nk * col_dev, targets, blk), f32)
+        scratch = [
+            pltpu.VMEM((boxes, targets, blk), f32),
+            pltpu.VMEM((boxes, targets, blk), f32),
+            dense, dense, dense,
+        ] + [dma((nd, nk))] * 4 + [dma((nk,))] * 4
         if first:
-            outs.append(shape(tags.shape, f32))
-            sems = sems + [pltpu.SemaphoreType.DMA((shards,))] * 2
+            outs += [shape(tags.shape, f32), shape((count_rows, blk), f32)]
+            counts = pltpu.VMEM((nk, count_rows, blk), f32)
+            scratch += [counts, counts, dma((nd,)), dma((nd,)), dma((nk,)), dma((nk,))]
+        if last:
+            specs[-2] = smem()
+            outs.append(shape((8, width), f32))
+            scratch += [pltpu.VMEM((shards, 8, width), f32), dma((shards,)), dma((shards,))]
+        mean_of = shards * local_cols * blk
         return pl.pallas_call(
-            functools.partial(agree_kernel, first, shards, capacity, col_dev),
+            functools.partial(agree_kernel, first, last, capacity, col_dev, mean_of),
             out_shape=tuple(outs),
-            in_specs=[vmem()] * 2,
+            in_specs=specs,
             out_specs=(vmem(),) * len(outs),
-            scratch_shapes=[
-                pltpu.VMEM((boxes, targets, blk), f32),
-                pltpu.VMEM((boxes, targets, blk), f32),
-            ] + sems,
+            scratch_shapes=scratch,
             compiler_params=pltpu.CompilerParams(
                 vmem_limit_bytes=big, has_side_effects=True
             ),
             name="agree",
-        )(box, tags)
+        )(*operands)
 
     for outer_step in range(ITERS):
         first, last = outer_step == 0, outer_step == ITERS - 1
+        operands = [box, tags]
+        if not first:
+            operands.append(share)
+        if last:
+            operands += [mailbox, x]
+        result = list(agree(first, last, *operands))
+        zbox, zown = result[:2]
         if first:
-            zbox, zown, tags = agree(True, box, tags)
-        else:
-            zbox, zown = agree(False, box, tags)
+            tags, share = result[2:4]
+        if last:
+            gap = result[-1]
         common = [
             pltpu.VMEM(vec, f32),
             pltpu.VMEM(vec, f32),
@@ -405,7 +573,7 @@
             pltpu.VMEM((row_blocks, 2 * targets, blk), b16),
         ]
         if last:
-            outs = (shape(vec, f32), shape(vec, f32), shape((targets, blk), f32))
+            outs = (shape(vec, f32), shape(vec, f32))
             common = [pltpu.VMEM(vec, f32)] + common
         else:
             outs = (
@@ -422,11 +590,10 @@
             name="solve",
         )(tile_row, tile_col, tile_count, mailbox, fwd, bwd, base, x, u, zbox)
         if last:
-            x, u, gap = result
+            x, u = result
         else:
             x, u, box, base = result
-    gap_total = lax.psum(jnp.sum(gap, axis=1), AXES)
-    primal_gap = jnp.sqrt(gap_total / (shards * local_cols * blk))
+    primal_gap = gap[0, :targets]
     return (jnp.swapaxes(x, 1, 2), jnp.swapaxes(u, 1, 2), jnp.swapaxes(zown, 1, 2), primal_gap)
 
 

time: 321 us -> 208 us (0.65)
  the two profiles are of different devices: /device:TPU:0 before, /device:TPU:7 now
where the time goes in v1:
time: 208 us; the launch traced here: 206 us
  Pallas kernels  193 us (93%)
  local copies, waits for them, and re-layouts  10.4 us (5%)
    pallas_call x2, Pallas kernels, agree(): pl.pallas_call(functools.partial(agree_kernel, first, last, capacity, col...  134 us
    pallas_call x2, Pallas kernels, on_device(): pl.pallas_call(functools.partial(solve_kernel, last), out_shape=outs, in_...  49.1 us
    pallas_call x1, Pallas kernels, on_device(): pl.pallas_call(prepare_kernel, out_shape=(shape((slots, 2 * blk, blk), b1...  10.6 us
    unnamed x19, local copies, waits for them, and re-layouts  9.66 us

profile of v1, /device:TPU:7, one launch (start us, length us, event | category | flops | bytes accessed | tf_op | source)
XLA Modules:
  0.0 206.2 jit_solution(11533024671909272491)
XLA Ops:
  1.3 0.8 select_reduce_fusion.1
  2.2 0.2 convert_reduce_fusion
  2.4 0.1 select_reduce_fusion
  2.5 0.1 convert_element_type.13
  2.6 0.1 broadcast_in_dim.12.refs_1_
  2.7 0.0 copy-start.2
  2.7 1.6 copy-done.2
  4.3 0.0 copy-start.4
  4.3 1.6 copy-done.4
  5.9 0.0 copy-start.6
  5.9 1.2 copy-done.6
  7.1 0.0 copy-start.7
  7.1 0.7 copy-done.7
  7.8 0.0 copy-start.8
  7.8 0.7 copy-done.8
  8.4 10.6 %prepare.1 = (bf16[64,256,128]{2,1,0:T(8,128)(2,1)S(1)}, bf16[64,256,128]{2,1,0:T(8,128)(2,1)}, f32[64,64,128]{2,1,0:T(8,128)S(1)}, f32[64,64,128]{2,1,0:T(8,128)S(1)}) custom-call(s32[1,64]{1,0:T(1,128)S(1)} %copy-done.7, s32[1,64]{1,0:T(1,128)S(1)} %copy-done.8, s32[1]{0:T(128)S(6)} %copy.14.count, s32[1,64]{1,0:T(1,128)S(1)} %bitcast_add_fusion.mailbox.refs_3_, ...), custom_call_target="tpu_custom_call" | custom-call | tf_op jit(solution)/shard_map/prepare/pallas_call | solution.py:501
  19.0 0.0 copy-start
  19.0 2.0 copy-done
  21.0 0.0 copy-start.3
  21.0 61.2 %agree.2 = (f32[64,64,128]{2,1,0:T(8,128)S(1)}, f32[4,64,128]{2,1,0:T(8,128)}, f32[32,8,128]{2,1,0:T(8,128)S(1)}, f32[8,128]{1,0:T(8,128)S(1)}) custom-call(f32[64,64,128]{2,1,0:T(8,128)S(1)} %get-tuple-element.23.refs_0_, f32[32,8,128]{2,1,0:T(8,128)S(1)} %broadcast_in_dim.12.refs_1_), custom_call_target="tpu_custom_call" | custom-call | tf_op jit(solution)/shard_map/agree/pallas_call | solution.py:543
  82.2 0.0 copy-start.5
  82.2 1.3 copy-done.5
  83.5 0.0 copy-done.3
  83.5 26.0 %solve.2 = (f32[64,64,128]{2,1,0:T(8,128)S(1)}, f32[64,64,128]{2,1,0:T(8,128)S(1)}, f32[64,64,128]{2,1,0:T(8,128)S(1)}, f32[64,64,128]{2,1,0:T(8,128)S(1)}) custom-call(s32[1,64]{1,0:T(1,128)S(1)} %copy-done.7, s32[1,64]{1,0:T(1,128)S(1)} %copy-done.8, s32[1]{0:T(128)S(6)} %copy.14.count, s32[1,64]{1,0:T(1,128)S(1)} %bitcast_add_fusion.mailbox.refs_3_, ...), custom_call_target="tpu_custom_call" | custom-call | tf_op jit(solution)/shard_map/solve/pallas_call | solution.py:583
  109.6 0.0 copy-start.1
  109.6 72.4 %agree.3 = (f32[64,64,128]{2,1,0:T(8,128)S(1)}, f32[4,64,128]{2,1,0:T(8,128)S(1)}, f32[8,128]{1,0:T(8,128)S(1)}) custom-call(f32[64,64,128]{2,1,0:T(8,128)S(1)} %get-tuple-element.28.refs_0_, f32[32,8,128]{2,1,0:T(8,128)S(1)} %get-tuple-element.29.refs_1_, f32[8,128]{1,0:T(8,128)S(1)} %get-tuple-element.30.refs_2_, ...), custom_call_target="tpu_custom_call" | custom-call | tf_op jit(solution)/shard_map/agree/pallas_call | solution.py:543
  182.0 0.0 copy-done.1
  182.0 23.1 %solve.3 = (f32[64,64,128]{2,1,0:T(8,128)}, f32[64,64,128]{2,1,0:T(8,128)}) custom-call(s32[1,64]{1,0:T(1,128)S(1)} %copy-done.7, s32[1,64]{1,0:T(1,128)S(1)} %copy-done.8, s32[1]{0:T(128)S(6)} %copy.14.count, s32[1,64]{1,0:T(1,128)S(1)} %bitcast_add_fusion.mailbox.refs_3_, bf16[64,256,128]{2,1,0:T(8,128)(2,1)S(1)} %copy-done.1, ...), custom_call_target="tpu_custom_call" | custom-call | tf_op jit(solution)/shard_map/solve/pallas_call | solution.py:583
  205.1 0.5 slice_bitcast_fusion
  205.6 0.7 copy.15
  (5 shorter events, 0.0 us)
Async XLA Ops:
  2.7 1.6 copy-start.2
  4.3 1.6 copy-start.4
  5.9 1.2 copy-start.6
  7.1 0.7 copy-start.7
  7.8 0.7 copy-start.8
  19.0 2.0 copy-start
  21.0 62.6 %copy-start.3 = (f32[64,128,64]{1,2,0:T(8,128)S(1)}, f32[64,128,64]{1,2,0:T(8,128)}, u32[]{:S(2)}) copy-start(f32[64,128,64]{1,2,0:T(8,128)} %param.16) | copy-start | bytes 6291460
  82.2 1.3 copy-start.5
  109.6 72.4 %copy-start.1 = (bf16[64,256,128]{2,1,0:T(8,128)(2,1)S(1)}, bf16[64,256,128]{2,1,0:T(8,128)(2,1)}, u32[]{:S(2)}) copy-start(bf16[64,256,128]{2,1,0:T(8,128)(2,1)} %copy-done) | copy-start | bytes 12582916
